TPU v7x, 256 devices: a 8x8x2 block of a 8x8x16 slice. The times are simulated.
256 devices in a mesh: slices: 2 (over z), wide: 16 (over y, core), narrow: 8 (over x).
Axes of the slice: x: 8, y: 8, z: 2, core: 2. Of those that a mesh axis runs over, the one named last changes fastest.
The devices are a block of a 8x8x16 slice.
Arguments:
- state: float32 [32, 8, 2, 16384], P(('slices', 'wide'), 'narrow'), parts along dimension 0, may hold values from -6 to 6
- gates: float32 [8, 7, 2, 4, 4], replicated, may hold values from -2 to 2
Outputs:
- final_state: float32 [32, 8, 2, 16384], P(('slices', 'wide'), 'narrow'), parts along dimension 0
- marginal: float32 [32, 16384], P(('slices', 'wide'), 'narrow'), parts along dimension 0
There are 2 independent parts, one for each index of `slices`. A program takes and returns all parts, laid end to end along the dimension named above; an argument that names none is the same for every part. Nothing has to cross between parts.
All inputs are finite; a program needn't handle non-finite values.
Results may differ from a plain program's by a relative error of at most 0.0003.
Values sent between devices are 32-bit elements; how exact they have to be, the bound alone decides.
No kernel may reach another device: no remote copies, remote signals or barrier semaphores. Data moves between devices by JAX's collectives and lax.ppermute only.
A program may use at most 192 MiB of HBM per device.

v0:
```python
import jax
import jax.numpy as jnp
from jax import lax
from jax.experimental import pallas as pl
from jax.experimental.pallas import tpu as pltpu
from jax.sharding import Mesh, PartitionSpec as P

RING = 21
STEP = 7
VREGS = 16
SUBLANES = 8
LANES = 128
TILE = (SUBLANES, LANES)


def pair_of(layer, low):
    return layer, ((low - layer * STEP) % RING) // 2


def lane_iota():
    return lax.broadcasted_iota(jnp.int32, TILE, 1)


def sublane_iota():
    return lax.broadcasted_iota(jnp.int32, TILE, 0)


def bit_of(array, place):
    return (array >> place) & 1


def splits(array):
    high = array.astype(jnp.bfloat16)
    low = (array - high.astype(jnp.float32)).astype(jnp.bfloat16)
    return high, low


def dot(a, b, dims):
    return lax.dot_general(a, b, (dims, ((), ())), preferred_element_type=jnp.float32)


def dot_three(a, b, dims):
    return dot(a[0], b[0], dims) + dot(a[0], b[1], dims) + dot(a[1], b[0], dims)


def stack(parts):
    return jnp.concatenate(parts, axis=0)


def beside(left, right):
    return tuple(jnp.concatenate([l, r], axis=1) for l, r in zip(left, right))


def over(top, bottom):
    return tuple(jnp.concatenate([t, b], axis=0) for t, b in zip(top, bottom))


def negative(parts):
    return tuple(-part for part in parts)


def unstack(array):
    return [array[SUBLANES * v : SUBLANES * (v + 1)] for v in range(array.shape[0] // SUBLANES)]


def times_from_left(matrix, real, imag):
    left = beside(splits(matrix[0]), splits(matrix[1]))
    re, im = splits(real), splits(imag)
    right = over(beside(re, im), beside(negative(im), re))
    out = dot_three(left, right, ((1,), (0,)))
    return out[:, :LANES], out[:, LANES:]


def lane_operator(matrix):
    re, im = splits(matrix[0]), splits(matrix[1])
    return over(beside(re, negative(im)), beside(im, re))


def times_on_lanes(operator, real, imag):
    out = dot_three(beside(splits(real), splits(imag)), operator, ((1,), (1,)))
    return out[:, :LANES], out[:, LANES:]


def times_on_lanes_transposed(operator, real, imag):
    out = dot_three(operator, beside(splits(real), splits(imag)), ((1,), (1,)))
    return out[:LANES], out[LANES:]


def table_of(gates_ref, scratch, layer, pair):
    at = 2 * (layer * gates_ref.shape[0] // 16 + pair)
    scratch[0:4, 0:4] = gates_ref[at]
    scratch[4:8, 0:4] = gates_ref[at + 1]
    return scratch[...]


def spread(tile, row):
    return jnp.broadcast_to(tile[row : row + 1, :], TILE)


def brick(gates, ins, outs):
    lane, sub = lane_iota(), sublane_iota()
    touched, factors = set(), []
    for table, low in gates:
        high = (low + 1) % RING
        touched |= {low, high}
        column = bit_of(lane, ins[low]) + 2 * bit_of(lane, ins[high])
        wide = jnp.take_along_axis(table, column, axis=1)
        factors.append((low, high, [(spread(wide, r), spread(wide, 4 + r)) for r in range(4)]))
    cache = {}

    def static(place, v):
        return None if place < 3 else (v >> (place - 3)) & 1

    def pick(place, v, zero, one):
        if place >= 3:
            return one if static(place, v) else zero
        mask = bit_of(sub, place) == 1
        return tuple(jnp.where(mask, o, z) for z, o in zip(zero, one))

    def entry(index, v):
        low, high, rows = factors[index]
        key = (index, static(outs[low], v), static(outs[high], v))
        if key not in cache:
            zero = pick(outs[low], v, rows[0], rows[1])
            one = pick(outs[low], v, rows[2], rows[3])
            cache[key] = pick(outs[high], v, zero, one)
        return cache[key], key

    real, imag = [], []
    for v in range(VREGS):
        value, key = entry(0, v)
        key = (key,)
        for index in range(1, len(factors)):
            other, own = entry(index, v)
            key = key + (own,)
            if key not in cache:
                (a, b), (c, d) = value, other
                cache[key] = (a * c - b * d, a * d + b * c)
            value = cache[key]
        mask = None
        for qubit in ins:
            if qubit in touched:
                continue
            place = outs[qubit]
            bit = bit_of(lane, ins[qubit])
            same = (bit == bit_of(sub, place)) if place < 3 else (bit == static(place, v))
            mask = same if mask is None else mask & same
        if mask is not None:
            value = tuple(jnp.where(mask, part, 0.0) for part in value)
        real.append(value[0])
        imag.append(value[1])
    return stack(real), stack(imag)


def product(layers, places, get, outs=None):
    matrix = None
    for number, layer in enumerate(layers):
        last = number == len(layers) - 1
        step = brick([(get(*g), g[1]) for g in layer], places, outs if outs and last else places)
        matrix = step if matrix is None else times_from_left(step, *matrix)
    return matrix


def flip_lanes(tile, place):
    width = 1 << place
    if 2 * width == LANES:
        return pltpu.roll(tile, width, 1)
    lane = lane_iota()
    return jnp.where(bit_of(lane, place) == 1, pltpu.roll(tile, width, 1), pltpu.roll(tile, LANES - width, 1))


def flip_rows(tiles, place):
    if place >= 3:
        return [tiles[v ^ (1 << (place - 3))] for v in range(VREGS)]
    width = 1 << place
    up = bit_of(sublane_iota(), place) == 1
    return [jnp.where(up, pltpu.roll(t, width, 0), pltpu.roll(t, SUBLANES - width, 0)) for t in tiles]


def cross(real, imag, table, lane_place, row_place, lane_is_low):
    lane, sub = lane_iota(), sublane_iota()
    lane_bit = bit_of(lane, lane_place)
    lane_weight, row_weight = (1, 2) if lane_is_low else (2, 1)

    def coefficient(row_value, row_flip, lane_flip):
        column = lane_weight * (lane_bit ^ lane_flip) + row_weight * (row_value ^ row_flip)
        wide = jnp.take_along_axis(table, column, axis=1)
        base = row_weight * row_value
        return tuple(
            jnp.where(lane_bit == 1, spread(wide, shift + base + lane_weight), spread(wide, shift + base))
            for shift in (0, 4)
        )

    def coefficients(row_value):
        return {(r, l): coefficient(row_value, r, l) for r in (0, 1) for l in (0, 1)}

    both = [coefficients(0), coefficients(1)]
    if row_place < 3:
        mask = bit_of(sub, row_place) == 1
        mixed = {k: tuple(jnp.where(mask, o, z) for z, o in zip(both[0][k], both[1][k])) for k in both[0]}
    inputs = {}
    for l in (0, 1):
        re = [flip_lanes(t, lane_place) for t in real] if l else real
        im = [flip_lanes(t, lane_place) for t in imag] if l else imag
        for r in (0, 1):
            inputs[r, l] = (flip_rows(re, row_place), flip_rows(im, row_place)) if r else (re, im)
    out_real, out_imag = [], []
    for v in range(VREGS):
        factors = mixed if row_place < 3 else both[(v >> (row_place - 3)) & 1]
        re = im = None
        for key, (c, d) in factors.items():
            a, b = inputs[key][0][v], inputs[key][1][v]
            re = a * c - b * d if re is None else re + a * c - b * d
            im = a * d + b * c if im is None else im + a * d + b * c
        out_real.append(re)
        out_imag.append(im)
    return out_real, out_imag


def exchanged(tiles, pairs):
    lane = lane_iota()
    for register, place in pairs:
        width = 1 << place
        upper = bit_of(lane, place) == 1
        result = list(tiles)
        for v in range(VREGS):
            if (v >> register) & 1:
                continue
            other = v | (1 << register)
            a, b = tiles[v], tiles[other]
            result[v] = jnp.where(upper, pltpu.roll(b, width, 1), a)
            result[other] = jnp.where(upper, b, pltpu.roll(a, LANES - width, 1))
        tiles = result
    return tiles


def places_of(qubits):
    return {q: place for place, q in enumerate(qubits)}


LANES_ONE, ROWS_ONE = places_of(range(0, 7)), places_of(range(7, 14))
LANES_TWO, ROWS_TWO = places_of([0, 1, 2, 3, 20, 19, 18]), places_of([14, 15, 16, 13, 12, 11, 17])
LANES_THREE, LANES_LAST = places_of([7, 8, 9, 13, 12, 11, 10]), places_of(range(7, 14))


def layers_of(*layers):
    return [[(layer, low) for layer, low in group] for group in layers]


A_ONE = layers_of(
    [(0, 0), (0, 2), (0, 4)], [(2, 1), (2, 3), (2, 5)], [(3, 2), (3, 4)], [(5, 3)]
)
B_ONE = layers_of(
    [(0, 8), (0, 10), (0, 12)], [(1, 7), (1, 9), (1, 11)], [(3, 8), (3, 10)], [(4, 9)]
)
A_ONE_LATE = layers_of([(5, 5)], [(6, 4)])
B_ONE_LATE = layers_of([(4, 7)], [(6, 8)])
A_TWO = layers_of([(1, 19)], [(2, 18), (2, 20)], [(4, 19), (3, 0)])
B_TWO = layers_of(
    [(1, 13), (1, 15)], [(2, 14), (2, 16), (3, 12)], [(4, 11), (4, 13), (4, 15)]
)
A_TWO_LATE = layers_of([(5, 18), (5, 20), (5, 1)], [(7, 19), (6, 0), (6, 2)])
B_TWO_LATE = layers_of([(5, 14), (5, 16), (6, 12)], [(7, 13), (7, 15)])
D_THREE = layers_of([(6, 10)], [(7, 9), (7, 11), (7, 7)])


def getter(gates_ref, scratch):
    def get(layer, low):
        return table_of(gates_ref, scratch, *pair_of(layer, low))

    return get


def pair_op(op, matrix, real, imag):
    re, im = op(matrix, stack(real), stack(imag))
    return unstack(re), unstack(im)


def stage_one(x_ref, gates_ref, out_ref, scratch):
    get = getter(gates_ref, scratch)
    real = [x_ref[pl.ds(16 * v, SUBLANES, stride=2), :] for v in range(VREGS)]
    imag = [x_ref[pl.ds(16 * v + 1, SUBLANES, stride=2), :] for v in range(VREGS)]
    real, imag = cross(real, imag, get(0, 6), 6, 0, True)
    real, imag = pair_op(times_on_lanes, lane_operator(product(A_ONE, LANES_ONE, get)), real, imag)
    real, imag = pair_op(times_from_left, product(B_ONE, ROWS_ONE, get), real, imag)
    real, imag = cross(real, imag, get(3, 6), 6, 0, True)
    real, imag = pair_op(times_on_lanes, lane_operator(product(A_ONE_LATE, LANES_ONE, get)), real, imag)
    real, imag = pair_op(times_from_left, product(B_ONE_LATE, ROWS_ONE, get), real, imag)
    real, imag = cross(real, imag, get(6, 6), 6, 0, True)
    pairs = ((3, 6), (2, 5), (1, 4))
    real, imag = exchanged(real, pairs), exchanged(imag, pairs)
    for v in range(VREGS):
        out_ref[pl.ds(16 * v, SUBLANES, stride=2), :] = real[v]
        out_ref[pl.ds(16 * v + 1, SUBLANES, stride=2), :] = imag[v]


def stage_two(x_ref, gates_ref, out_ref, scratch):
    get = getter(gates_ref, scratch)
    real = [x_ref[pl.ds(16 * v, SUBLANES, stride=2), :] for v in range(VREGS)]
    imag = [x_ref[pl.ds(16 * v + 1, SUBLANES, stride=2), :] for v in range(VREGS)]
    pairs = ((1, 6), (2, 5), (3, 4))
    real, imag = exchanged(real, pairs), exchanged(imag, pairs)
    order = [((v << 1) & 15) | (v >> 3) for v in range(VREGS)]
    real, imag = [real[o] for o in order], [imag[o] for o in order]
    real, imag = cross(real, imag, get(1, 17), 6, 6, False)
    real, imag = pair_op(times_on_lanes, lane_operator(product(A_TWO, LANES_TWO, get)), real, imag)
    real, imag = pair_op(times_from_left, product(B_TWO, ROWS_TWO, get), real, imag)
    real, imag = cross(real, imag, get(4, 17), 6, 6, False)
    real, imag = pair_op(times_from_left, product(B_TWO_LATE, ROWS_TWO, get), real, imag)
    late = lane_operator(product(A_TWO_LATE, LANES_TWO, get))
    real, imag = pair_op(times_on_lanes_transposed, late, real, imag)
    real, imag = cross(real, imag, get(7, 17), 6, 6, True)
    for v in range(VREGS):
        three, q20, q19, q18 = v & 1, (v >> 1) & 1, (v >> 2) & 1, v >> 3
        at = 32 * (8 * three + 4 * q20 + 2 * q19 + q18) + 16
        out_ref[at : at + 8, :] = real[v]
        out_ref[at + 8 : at + 16, :] = imag[v]
    for three in range(2):
        for part in range(2):
            for low in range(SUBLANES):
                to = 32 * (8 * three + low) + 8 * part
                rows = out_ref[pl.ds(256 * three + 16 + 8 * part + low, SUBLANES, stride=32), :]
                out_ref[to : to + 8, :] = rows


def stage_three(x_ref, gates_ref, state_ref, marginal_ref, scratch):
    get = getter(gates_ref, scratch)
    operator = lane_operator(product(D_THREE, LANES_THREE, get, LANES_LAST))
    pairs = ((3, 6), (2, 2), (1, 1), (0, 0))
    for layout in range(2):
        real = [x_ref[32 * v + 16 * layout : 32 * v + 16 * layout + 8, :] for v in range(VREGS)]
        imag = [x_ref[32 * v + 16 * layout + 8 : 32 * v + 16 * layout + 16, :] for v in range(VREGS)]
        real, imag = exchanged(real, pairs), exchanged(imag, pairs)
        real, imag = pair_op(times_on_lanes, operator, real, imag)
        for v in range(VREGS):
            if layout == 0:
                state_ref[pl.ds(2 * v, SUBLANES, stride=32), :] = real[v]
                state_ref[pl.ds(2 * v + 1, SUBLANES, stride=32), :] = imag[v]
            else:
                prob = real[v] * real[v] + imag[v] * imag[v]
                marginal_ref[v : v + 1, :] = jnp.sum(prob, axis=0, keepdims=True)


INTERPRET = False


def run(kernel, shapes, x, gates, name):
    return pl.pallas_call(
        kernel,
        out_shape=[jax.ShapeDtypeStruct(shape, jnp.float32) for shape in shapes],
        scratch_shapes=[pltpu.VMEM(TILE, jnp.float32)],
        name=name,
        interpret=INTERPRET,
    )(x, gates)


def first(x, gates):
    return run(stage_one, [(256, LANES)], x, gates, "stage_one")[0]


def second(x, gates):
    return run(stage_two, [(512, LANES)], x, gates, "stage_two")[0]


def third(x, gates):
    return run(stage_three, [(256, LANES), (16, LANES)], x, gates, "stage_three")


def local(state, gates):
    amplitudes = state.shape[-1]
    rows = amplitudes // LANES
    matrices = gates.reshape(-1, *gates.shape[-2:])
    x = state.reshape(2, rows, LANES).transpose(1, 0, 2).reshape(2 * rows, LANES)
    x = first(x, matrices)
    x = lax.all_to_all(x, ("high", "core", "narrow"), 0, 0, tiled=True)
    x = second(x, matrices)
    x = lax.all_to_all(x, ("core", "narrow"), 0, 0, tiled=True)
    final, marginal = third(x, matrices)
    final = final.reshape(rows, 2, LANES).transpose(1, 0, 2)
    return final.reshape(1, 1, 2, amplitudes), marginal.reshape(1, -1)


def solution(mesh):
    slices, wide, narrow = mesh.devices.shape
    devices = mesh.devices.reshape(slices, wide // 2, 2, narrow)
    split = Mesh(devices, ("slices", "high", "core", "narrow"))
    over_wide = ("slices", "high", "core")
    spec = P(over_wide, "narrow", None, None)
    return jax.shard_map(
        local, mesh=split, in_specs=(spec, P()), out_specs=(spec, P(over_wide, "narrow")), check_vma=False
    )
```

profile of v0, /device:TPU:513, one launch (start us, length us, event | category | flops | bytes accessed | tf_op | source)
XLA Modules:
  0.0 67.8 jit_solution(8269539816836097703)
XLA Ops:
  0.6 2.0 %copy.5 = f32[8,7,2,4,4]{4,3,2,1,0:T(4,128)} copy(f32[8,7,2,4,4]{0,4,3,2,1:T(4,128)} %param.3) | data formatting | bytes 14336 | tf_op args[1]
  2.6 4.2 %stage_one.1 = f32[256,128]{1,0:T(8,128)} custom-call(f32[256,128]{1,0:T(8,128)} %bitcast.23, f32[112,4,4]{2,1,0:T(4,128)} %bitcast.16), custom_call_target="tpu_custom_call" | custom-call | tf_op jit(solution)/shard_map/stage_one/pallas_call | solution.py:348
  6.8 40.7 %all_to_all.22 = f32[128,2,128]{2,1,0:T(2,128)} all-to-all(f32[128,2,128]{2,1,0:T(2,128)} %bitcast.22), channel_id=1, replica_groups=mesh['slices'=2,'high'=8,'core'=2,'narrow'=8] {'high','core','narrow'}, dimensions={0} | all-to-all | bytes 262144 | tf_op jit(solution)/shard_map/all_to_all | solution.py:375
  47.5 3.8 %stage_two.1 = f32[512,128]{1,0:T(8,128)} custom-call(f32[256,128]{1,0:T(8,128)} %bitcast.21, f32[112,4,4]{2,1,0:T(4,128)} %bitcast.17), custom_call_target="tpu_custom_call" | custom-call | tf_op jit(solution)/shard_map/stage_two/pallas_call | solution.py:348
  51.4 14.0 %all_to_all.23 = f32[16,32,128]{2,1,0:T(8,128)} all-to-all(f32[16,32,128]{2,1,0:T(8,128)} %bitcast.19), channel_id=1, replica_groups=mesh['slices'=2,'high'=8,'core'=2,'narrow'=8] {'core','narrow'}, dimensions={0} | all-to-all | bytes 524288 | tf_op jit(solution)/shard_map/all_to_all | solution.py:377
  65.4 2.4 %stage_three.1 = (f32[256,128]{1,0:T(8,128)}, f32[16,128]{1,0:T(8,128)}) custom-call(f32[512,128]{1,0:T(8,128)} %bitcast.20, f32[112,4,4]{2,1,0:T(4,128)} %bitcast.18), custom_call_target="tpu_custom_call" | custom-call | tf_op jit(solution)/shard_map/stage_three/pallas_call | solution.py:348
where the time goes:
time: 68.6 us; the launch traced here: 67.8 us
  blocking collectives  54.7 us (80%)
  Pallas kernels  10.5 us (15%)
  local copies, waits for them, and re-layouts  1.98 us (3%)
    all_to_all x1, blocking collectives, local(): x = lax.all_to_all(x, ('high', 'core', 'narrow'), 0, 0, tiled=True)  40.7 us
    all_to_all x1, blocking collectives, local(): x = lax.all_to_all(x, ('core', 'narrow'), 0, 0, tiled=True)  14 us
    pallas_call x3, Pallas kernels, run(): pl.pallas_call(kernel, out_shape=[jax.ShapeDtypeStruct(shape, jnp.float32...  10.5 us
    unnamed x1, local copies, waits for them, and re-layouts  1.98 us

commit v1 on v0

--- a/solution.py
+++ b/solution.py
@@ -13,10 +13,6 @@
 TILE = (SUBLANES, LANES)
 
 
-def pair_of(layer, low):
-    return layer, ((low - layer * STEP) % RING) // 2
-
-
 def lane_iota():
     return lax.broadcasted_iota(jnp.int32, TILE, 1)
 
@@ -86,15 +82,19 @@
     return out[:LANES], out[LANES:]
 
 
-def table_of(gates_ref, scratch, layer, pair):
-    at = 2 * (layer * gates_ref.shape[0] // 16 + pair)
-    scratch[0:4, 0:4] = gates_ref[at]
-    scratch[4:8, 0:4] = gates_ref[at + 1]
-    return scratch[...]
+def gate_tiles(gates_ref):
+    rows = gates_ref.shape[0]
+    tail = jnp.concatenate([gates_ref[LANES:, :], jnp.zeros((2 * LANES - rows, SUBLANES), jnp.float32)], axis=0)
+    return gates_ref[:LANES, :].T, tail.T
 
 
 def spread(tile, row):
     return jnp.broadcast_to(tile[row : row + 1, :], TILE)
+
+
+def column_tile(gate, column):
+    tile, base = gate
+    return jnp.take_along_axis(tile, base + 4 * sublane_iota() + column, axis=1)
 
 
 def brick(gates, ins, outs):
@@ -104,7 +104,7 @@
         high = (low + 1) % RING
         touched |= {low, high}
         column = bit_of(lane, ins[low]) + 2 * bit_of(lane, ins[high])
-        wide = jnp.take_along_axis(table, column, axis=1)
+        wide = column_tile(table, column)
         factors.append((low, high, [(spread(wide, r), spread(wide, 4 + r)) for r in range(4)]))
     cache = {}
 
@@ -184,7 +184,7 @@
 
     def coefficient(row_value, row_flip, lane_flip):
         column = lane_weight * (lane_bit ^ lane_flip) + row_weight * (row_value ^ row_flip)
-        wide = jnp.take_along_axis(table, column, axis=1)
+        wide = column_tile(table, column)
         base = row_weight * row_value
         return tuple(
             jnp.where(lane_bit == 1, spread(wide, shift + base + lane_weight), spread(wide, shift + base))
@@ -264,9 +264,12 @@
 D_THREE = layers_of([(6, 10)], [(7, 9), (7, 11), (7, 7)])
 
 
-def getter(gates_ref, scratch):
+def getter(gates_ref):
+    tiles = gate_tiles(gates_ref)
+
     def get(layer, low):
-        return table_of(gates_ref, scratch, *pair_of(layer, low))
+        pair = ((low - layer * STEP) % RING) // 2
+        return spread(tiles[pair // 4], layer), 32 * (pair % 4)
 
     return get
 
@@ -276,8 +279,8 @@
     return unstack(re), unstack(im)
 
 
-def stage_one(x_ref, gates_ref, out_ref, scratch):
-    get = getter(gates_ref, scratch)
+def stage_one(x_ref, gates_ref, out_ref):
+    get = getter(gates_ref)
     real = [x_ref[pl.ds(16 * v, SUBLANES, stride=2), :] for v in range(VREGS)]
     imag = [x_ref[pl.ds(16 * v + 1, SUBLANES, stride=2), :] for v in range(VREGS)]
     real, imag = cross(real, imag, get(0, 6), 6, 0, True)
@@ -294,8 +297,8 @@
         out_ref[pl.ds(16 * v + 1, SUBLANES, stride=2), :] = imag[v]
 
 
-def stage_two(x_ref, gates_ref, out_ref, scratch):
-    get = getter(gates_ref, scratch)
+def stage_two(x_ref, gates_ref, out_ref):
+    get = getter(gates_ref)
     real = [x_ref[pl.ds(16 * v, SUBLANES, stride=2), :] for v in range(VREGS)]
     imag = [x_ref[pl.ds(16 * v + 1, SUBLANES, stride=2), :] for v in range(VREGS)]
     pairs = ((1, 6), (2, 5), (3, 4))
@@ -323,8 +326,8 @@
                 out_ref[to : to + 8, :] = rows
 
 
-def stage_three(x_ref, gates_ref, state_ref, marginal_ref, scratch):
-    get = getter(gates_ref, scratch)
+def stage_three(x_ref, gates_ref, state_ref, marginal_ref):
+    get = getter(gates_ref)
     operator = lane_operator(product(D_THREE, LANES_THREE, get, LANES_LAST))
     pairs = ((3, 6), (2, 2), (1, 1), (0, 0))
     for layout in range(2):
@@ -342,13 +345,14 @@
 
 
 INTERPRET = False
+VMEM_LIMIT = 8 << 20
 
 
 def run(kernel, shapes, x, gates, name):
     return pl.pallas_call(
         kernel,
         out_shape=[jax.ShapeDtypeStruct(shape, jnp.float32) for shape in shapes],
-        scratch_shapes=[pltpu.VMEM(TILE, jnp.float32)],
+        compiler_params=pltpu.CompilerParams(vmem_limit_bytes=VMEM_LIMIT),
         name=name,
         interpret=INTERPRET,
     )(x, gates)
@@ -369,7 +373,7 @@
 def local(state, gates):
     amplitudes = state.shape[-1]
     rows = amplitudes // LANES
-    matrices = gates.reshape(-1, *gates.shape[-2:])
+    matrices = gates.transpose(1, 2, 3, 4, 0).reshape(-1, gates.shape[0])
     x = state.reshape(2, rows, LANES).transpose(1, 0, 2).reshape(2 * rows, LANES)
     x = first(x, matrices)
     x = lax.all_to_all(x, ("high", "core", "narrow"), 0, 0, tiled=True)

time: 68.6 us -> 61.3 us (0.89)
  Pallas kernels: 10.5 us -> 6.45 us
  blocking collectives: 54.7 us -> 52 us
    pallas_call x3, Pallas kernels: 10.5 us -> 6.45 us  [run(): pl.pallas_call(kernel, out_shape=[jax.ShapeDtypeStruct(shape, jnp.float32...]
    all_to_all x1, blocking collectives: 40.7 us -> 39.2 us  [local(): x = lax.all_to_all(x, ('high', 'core', 'narrow'), 0, 0, tiled=True)]
    all_to_all x1, blocking collectives: 14 us -> 12.7 us  [local(): x = lax.all_to_all(x, ('core', 'narrow'), 0, 0, tiled=True)]
    unnamed x1 -> x6, local copies, waits for them, and re-layouts: 1.98 us -> 1.8 us
where the time goes in v1:
time: 61.3 us; the launch traced here: 60.9 us
  blocking collectives  52 us (85%)
  Pallas kernels  6.45 us (11%)
  local copies, waits for them, and re-layouts  1.8 us (3%)
  between operations  0.66 us (1%)
    all_to_all x1, blocking collectives, local(): x = lax.all_to_all(x, ('high', 'core', 'narrow'), 0, 0, tiled=True)  39.2 us
    all_to_all x1, blocking collectives, local(): x = lax.all_to_all(x, ('core', 'narrow'), 0, 0, tiled=True)  12.7 us
    pallas_call x3, Pallas kernels, run(): pl.pallas_call(kernel, out_shape=[jax.ShapeDtypeStruct(shape, jnp.float32...  6.45 us
    unnamed x6, local copies, waits for them, and re-layouts  1.8 us

profile of v1, /device:TPU:513, one launch (start us, length us, event | category | flops | bytes accessed | tf_op | source)
XLA Modules:
  0.0 60.9 jit_solution(15505362443896543276)
XLA Ops:
  0.6 0.0 copy-start
  0.6 0.9 %copy-done = f32[8,7,2,4,4]{0,4,3,2,1:T(4,128)S(1)} copy-done((f32[8,7,2,4,4]{0,4,3,2,1:T(4,128)S(1)}, f32[8,7,2,4,4]{0,4,3,2,1:T(4,128)}, u32[]{:S(2)}) %copy-start) | copy-done | bytes 7192
  1.5 0.0 copy-start.2
  1.5 0.9 %copy-done.2 = f32[1,1,2,16384]{3,2,1,0:T(2,128)S(1)} copy-done((f32[1,1,2,16384]{3,2,1,0:T(2,128)S(1)}, f32[1,1,2,16384]{3,2,1,0:T(2,128)}, u32[]{:S(2)}) %copy-start.2) | copy-done | bytes 131096
  2.4 2.7 %stage_one.1 = f32[256,128]{1,0:T(8,128)S(1)} custom-call(f32[256,128]{1,0:T(8,128)S(1)} %bitcast.25, f32[224,8]{1,0:T(8,128)S(1)} %bitcast.20), custom_call_target="tpu_custom_call" | custom-call | tf_op jit(solution)/shard_map/stage_one/pallas_call | solution.py:352
  5.1 0.0 copy-start.1
  5.1 39.2 %all_to_all.22 = f32[128,2,128]{2,1,0:T(2,128)S(1)} all-to-all(f32[128,2,128]{2,1,0:T(2,128)S(1)} %bitcast.23), channel_id=1, replica_groups=mesh['slices'=2,'high'=8,'core'=2,'narrow'=8] {'high','core','narrow'}, dimensions={0} | all-to-all | bytes 262144 | tf_op jit(solution)/shard_map/all_to_all | solution.py:379
  44.3 0.0 copy-done.1
  44.4 2.3 %stage_two.1 = f32[512,128]{1,0:T(8,128)S(1)} custom-call(f32[256,128]{1,0:T(8,128)S(1)} %bitcast.24, f32[224,8]{1,0:T(8,128)S(1)} %bitcast.21), custom_call_target="tpu_custom_call" | custom-call | tf_op jit(solution)/shard_map/stage_two/pallas_call | solution.py:352
  46.6 12.7 %all_to_all.23 = f32[16,32,128]{2,1,0:T(8,128)S(1)} all-to-all(f32[16,32,128]{2,1,0:T(8,128)S(1)} %bitcast.19), channel_id=1, replica_groups=mesh['slices'=2,'high'=8,'core'=2,'narrow'=8] {'core','narrow'}, dimensions={0} | all-to-all | bytes 524288 | tf_op jit(solution)/shard_map/all_to_all | solution.py:381
  59.3 1.5 %stage_three.1 = (f32[256,128]{1,0:T(8,128)}, f32[16,128]{1,0:T(8,128)}) custom-call(f32[512,128]{1,0:T(8,128)S(1)} %bitcast.18, f32[224,8]{1,0:T(8,128)S(1)} %bitcast.22), custom_call_target="tpu_custom_call" | custom-call | tf_op jit(solution)/shard_map/stage_three/pallas_call | solution.py:352
Async XLA Ops:
  0.6 0.9 %copy-start = (f32[8,7,2,4,4]{0,4,3,2,1:T(4,128)S(1)}, f32[8,7,2,4,4]{0,4,3,2,1:T(4,128)}, u32[]{:S(2)}) copy-start(f32[8,7,2,4,4]{0,4,3,2,1:T(4,128)} %param.3) | copy-start | bytes 21508
  1.5 0.9 %copy-start.2 = (f32[1,1,2,16384]{3,2,1,0:T(2,128)S(1)}, f32[1,1,2,16384]{3,2,1,0:T(2,128)}, u32[]{:S(2)}) copy-start(f32[1,1,2,16384]{3,2,1,0:T(2,128)} %param.2) | copy-start | bytes 393220
  5.1 39.3 %copy-start.1 = (f32[8,7,2,4,4]{0,4,3,2,1:T(4,128)S(1)}, f32[8,7,2,4,4]{0,4,3,2,1:T(4,128)}, u32[]{:S(2)}) copy-start(f32[8,7,2,4,4]{0,4,3,2,1:T(4,128)} %param.3) | copy-start | bytes 21508

commit v2 on v1

v2 whole, which is shorter than its diff:
```python
import jax
import jax.numpy as jnp
from jax import lax
from jax.experimental import pallas as pl
from jax.experimental.pallas import tpu as pltpu
from jax.sharding import Mesh, PartitionSpec as P

RING = 21
STEP = 7
VREGS = 16
SUBLANES = 8
LANES = 128
TILE = (SUBLANES, LANES)
LEFT = ((1,), (0,))
RIGHT = ((1,), (1,))


def lane_iota():
    return lax.broadcasted_iota(jnp.int32, TILE, 1)


def sublane_iota():
    return lax.broadcasted_iota(jnp.int32, TILE, 0)


def bit_of(array, place):
    return (array >> place) & 1


def splits(array):
    high = array.astype(jnp.bfloat16)
    low = (array - high.astype(jnp.float32)).astype(jnp.bfloat16)
    return high, low


def dot(a, b, dims):
    return lax.dot_general(a, b, (dims, ((), ())), preferred_element_type=jnp.float32)


def dot_three(a, b, dims):
    return dot(a[0], b[0], dims) + dot(a[0], b[1], dims) + dot(a[1], b[0], dims)


def stack(parts):
    return jnp.concatenate(parts, axis=0)


def beside(left, right):
    return tuple(jnp.concatenate([l, r], axis=1) for l, r in zip(left, right))


def over(top, bottom):
    return tuple(jnp.concatenate([t, b], axis=0) for t, b in zip(top, bottom))


def negative(parts):
    return tuple(-part for part in parts)


def unstack(array):
    return [array[SUBLANES * v : SUBLANES * (v + 1)] for v in range(array.shape[0] // SUBLANES)]


def row_operator(matrix):
    return beside(splits(matrix[0]), splits(matrix[1]))


def lane_operator(matrix):
    re, im = splits(matrix[0]), splits(matrix[1])
    return over(beside(re, negative(im)), beside(im, re))


def times_on_rows(operator, real, imag):
    re, im = splits(real), splits(imag)
    out = dot_three(operator, over(beside(re, im), beside(negative(im), re)), LEFT)
    return out[:, :LANES], out[:, LANES:]


def times_on_lanes(operator, real, imag):
    out = dot_three(beside(splits(real), splits(imag)), operator, RIGHT)
    return out[:, :LANES], out[:, LANES:]


def times_on_lanes_transposed(operator, real, imag):
    out = dot_three(operator, beside(splits(real), splits(imag)), RIGHT)
    return out[:LANES], out[LANES:]


def gate_tiles(gates_ref):
    rows = gates_ref.shape[0]
    tail = jnp.concatenate([gates_ref[LANES:, :], jnp.zeros((2 * LANES - rows, SUBLANES), jnp.float32)], axis=0)
    return gates_ref[:LANES, :].T, tail.T


def column_tile(gate, column):
    tile, base = gate
    return jnp.take_along_axis(tile, base + 4 * sublane_iota() + column, axis=1)


def spread(tile, row):
    return jnp.broadcast_to(tile[row : row + 1, :], TILE)


def getter(gates_ref):
    tiles = gate_tiles(gates_ref)

    def get(layer, low):
        pair = ((low - layer * STEP) % RING) // 2
        return spread(tiles[pair // 4], layer), 32 * (pair % 4)

    return get


def brick(gates, ins, outs):
    lane, sub = lane_iota(), sublane_iota()
    touched, factors = set(), []
    for gate, low in gates:
        high = (low + 1) % RING
        touched |= {low, high}
        wide = column_tile(gate, bit_of(lane, ins[low]) + 2 * bit_of(lane, ins[high]))
        factors.append((low, high, [(spread(wide, r), spread(wide, 4 + r)) for r in range(4)]))
    cache = {}

    def static(place, v):
        return None if place < 3 else (v >> (place - 3)) & 1

    def pick(place, v, zero, one):
        if place >= 3:
            return one if static(place, v) else zero
        mask = bit_of(sub, place) == 1
        return tuple(jnp.where(mask, o, z) for z, o in zip(zero, one))

    def entry(index, v):
        low, high, rows = factors[index]
        key = (index, static(outs[low], v), static(outs[high], v))
        if key not in cache:
            zero = pick(outs[low], v, rows[0], rows[1])
            one = pick(outs[low], v, rows[2], rows[3])
            cache[key] = pick(outs[high], v, zero, one)
        return cache[key], key

    real, imag = [], []
    for v in range(VREGS):
        value, key = entry(0, v)
        key = (key,)
        for index in range(1, len(factors)):
            other, own = entry(index, v)
            key = key + (own,)
            if key not in cache:
                (a, b), (c, d) = value, other
                cache[key] = (a * c - b * d, a * d + b * c)
            value = cache[key]
        mask = None
        for qubit in ins:
            if qubit in touched:
                continue
            place = outs[qubit]
            bit = bit_of(lane, ins[qubit])
            same = (bit == bit_of(sub, place)) if place < 3 else (bit == static(place, v))
            mask = same if mask is None else mask & same
        if mask is not None:
            value = tuple(jnp.where(mask, part, 0.0) for part in value)
        real.append(value[0])
        imag.append(value[1])
    return stack(real), stack(imag)


def products(get, *groups):
    chains = []
    for layers, ins, outs in groups:
        last = len(layers) - 1
        chains.append(
            [brick([(get(*g), g[1]) for g in layer], ins, outs if n == last else ins) for n, layer in enumerate(layers)]
        )
    while any(len(chain) > 1 for chain in chains):
        for number, chain in enumerate(chains):
            joined = [
                times_on_rows(row_operator(chain[i + 1]), *chain[i]) if i + 1 < len(chain) else chain[i]
                for i in range(0, len(chain), 2)
            ]
            chains[number] = joined
    return [chain[0] for chain in chains]


def flip_lanes(tile, place):
    width = 1 << place
    if 2 * width == LANES:
        return pltpu.roll(tile, width, 1)
    lane = lane_iota()
    return jnp.where(bit_of(lane, place) == 1, pltpu.roll(tile, width, 1), pltpu.roll(tile, LANES - width, 1))


def flip_rows(tiles, place):
    if place >= 3:
        return [tiles[v ^ (1 << (place - 3))] for v in range(VREGS)]
    width = 1 << place
    up = bit_of(sublane_iota(), place) == 1
    return [jnp.where(up, pltpu.roll(t, width, 0), pltpu.roll(t, SUBLANES - width, 0)) for t in tiles]


FLIPS = ((0, 0), (0, 1), (1, 0), (1, 1))


def cross_coefficients(gate, lane_place, row_place, lane_is_low):
    lane_bit = bit_of(lane_iota(), lane_place)
    lane_weight, row_weight = (1, 2) if lane_is_low else (2, 1)

    def coefficient(row_value, row_flip, lane_flip):
        column = lane_weight * (lane_bit ^ lane_flip) + row_weight * (row_value ^ row_flip)
        wide = column_tile(gate, column)
        base = row_weight * row_value
        return tuple(
            jnp.where(lane_bit == 1, spread(wide, shift + base + lane_weight), spread(wide, shift + base))
            for shift in (0, 4)
        )

    both = [[coefficient(value, *flips) for flips in FLIPS] for value in (0, 1)]
    if row_place < 3:
        mask = bit_of(sublane_iota(), row_place) == 1
        mixed = [tuple(jnp.where(mask, o, z) for z, o in zip(*pair)) for pair in zip(*both)]
        return [mixed, mixed]
    return both


def cross(real, imag, factors, lane_place, row_place):
    inputs = []
    lanes = (real, imag), tuple([flip_lanes(t, lane_place) for t in part] for part in (real, imag))
    for row_flip, lane_flip in FLIPS:
        parts = lanes[lane_flip]
        inputs.append(tuple(flip_rows(part, row_place) for part in parts) if row_flip else parts)
    out_real, out_imag = [], []
    for v in range(VREGS):
        re = im = None
        for (c, d), (xs, ys) in zip(factors[(v >> (row_place - 3)) & 1 if row_place >= 3 else 0], inputs):
            a, b = xs[v], ys[v]
            re = a * c - b * d if re is None else re + a * c - b * d
            im = a * d + b * c if im is None else im + a * d + b * c
        out_real.append(re)
        out_imag.append(im)
    return out_real, out_imag


def exchanged(tiles, pairs):
    lane = lane_iota()
    uppers = [bit_of(lane, place) == 1 for _, place in pairs]
    count = 1 << len(pairs)
    result = []
    for v in range(VREGS):
        base, shift = v, 0
        for register, place in pairs:
            if (v >> register) & 1:
                base ^= 1 << register
                shift -= 1 << place
        parts = []
        for group in range(count):
            source, move = base, shift
            for number, (register, place) in enumerate(pairs):
                if (group >> number) & 1:
                    source |= 1 << register
                    move += 1 << place
            move %= LANES
            parts.append(pltpu.roll(tiles[source], move, 1) if move else tiles[source])
        for upper in uppers:
            parts = [jnp.where(upper, parts[i + 1], parts[i]) for i in range(0, len(parts), 2)]
        result.append(parts[0])
    return result


def places_of(qubits):
    return {q: place for place, q in enumerate(qubits)}


LANES_ONE, ROWS_ONE = places_of(range(0, 7)), places_of(range(7, 14))
LANES_TWO, ROWS_TWO = places_of([0, 1, 2, 3, 20, 19, 18]), places_of([14, 15, 16, 13, 12, 11, 17])
LANES_THREE, LANES_LAST = places_of([7, 8, 9, 13, 12, 11, 10]), places_of(range(7, 14))

A_ONE = [[(0, 0), (0, 2), (0, 4)], [(2, 1), (2, 3), (2, 5)], [(3, 2), (3, 4)], [(5, 3)]]
B_ONE = [[(0, 8), (0, 10), (0, 12)], [(1, 7), (1, 9), (1, 11)], [(3, 8), (3, 10)], [(4, 9)]]
A_ONE_LATE = [[(5, 5)], [(6, 4)]]
B_ONE_LATE = [[(4, 7)], [(6, 8)]]
A_TWO = [[(1, 19)], [(2, 18), (2, 20)], [(4, 19), (3, 0)]]
B_TWO = [[(1, 13), (1, 15)], [(2, 14), (2, 16), (3, 12)], [(4, 11), (4, 13), (4, 15)]]
A_TWO_LATE = [[(5, 18), (5, 20), (5, 1)], [(7, 19), (6, 0), (6, 2)]]
B_TWO_LATE = [[(5, 14), (5, 16), (6, 12)], [(7, 13), (7, 15)]]
D_THREE = [[(6, 10)], [(7, 9), (7, 11), (7, 7)]]


def pair_op(op, operator, real, imag):
    re, im = op(operator, stack(real), stack(imag))
    return unstack(re), unstack(im)


def rows_of(ref):
    return (
        [ref[pl.ds(16 * v, SUBLANES, stride=2), :] for v in range(VREGS)],
        [ref[pl.ds(16 * v + 1, SUBLANES, stride=2), :] for v in range(VREGS)],
    )


def stage_one(state_ref, gates_hbm, out_ref, x_ref, gates_ref, semaphores):
    gates_copy = pltpu.make_async_copy(gates_hbm, gates_ref, semaphores.at[0])
    state_copy = pltpu.make_async_copy(state_ref, x_ref, semaphores.at[1])
    gates_copy.start()
    state_copy.start()
    gates_copy.wait()
    state_copy.wait()
    get = getter(gates_ref)
    lanes, rows = (LANES_ONE, LANES_ONE), (ROWS_ONE, ROWS_ONE)
    a, b, a_late, b_late = products(
        get, (A_ONE, *lanes), (B_ONE, *rows), (A_ONE_LATE, *lanes), (B_ONE_LATE, *rows)
    )
    real, imag = rows_of(x_ref)
    real, imag = cross(real, imag, cross_coefficients(get(0, 6), 6, 0, True), 6, 0)
    real, imag = pair_op(times_on_lanes, lane_operator(a), real, imag)
    real, imag = pair_op(times_on_rows, row_operator(b), real, imag)
    real, imag = cross(real, imag, cross_coefficients(get(3, 6), 6, 0, True), 6, 0)
    real, imag = pair_op(times_on_lanes, lane_operator(a_late), real, imag)
    real, imag = pair_op(times_on_rows, row_operator(b_late), real, imag)
    real, imag = cross(real, imag, cross_coefficients(get(6, 6), 6, 0, True), 6, 0)
    pairs = ((3, 6), (2, 5), (1, 4))
    real, imag = exchanged(real, pairs), exchanged(imag, pairs)
    for v in range(VREGS):
        out_ref[pl.ds(16 * v, SUBLANES, stride=2), :] = real[v]
        out_ref[pl.ds(16 * v + 1, SUBLANES, stride=2), :] = imag[v]


CROSSES_TWO = (((1, 17), False), ((4, 17), False), ((7, 17), True))


def operators(gates_ref, after_ref, a_ref, b_ref, a_late_ref, b_late_ref, d_ref, factors_ref):
    get = getter(gates_ref)
    lanes, rows = (LANES_TWO, LANES_TWO), (ROWS_TWO, ROWS_TWO)
    a, b, a_late, b_late, d = products(
        get,
        (A_TWO, *lanes),
        (B_TWO, *rows),
        (A_TWO_LATE, *lanes),
        (B_TWO_LATE, *rows),
        (D_THREE, LANES_THREE, LANES_LAST),
    )
    for ref, value in (
        (a_ref, lane_operator(a)),
        (b_ref, row_operator(b)),
        (a_late_ref, lane_operator(a_late)),
        (b_late_ref, row_operator(b_late)),
        (d_ref, lane_operator(d)),
    ):
        for part in range(2):
            ref[part] = value[part]
    at = 0
    for gate, lane_is_low in CROSSES_TWO:
        for value in cross_coefficients(get(*gate), 6, 6, lane_is_low):
            for pair in value:
                for tile in pair:
                    factors_ref[at : at + SUBLANES, :] = tile
                    at += SUBLANES


def factors_of(ref, number):
    tiles = iter(ref[at : at + SUBLANES, :] for at in range(LANES * number, LANES * (number + 1), SUBLANES))
    return [[(next(tiles), next(tiles)) for _ in FLIPS] for _ in range(2)]


def stage_two(x_ref, a_ref, b_ref, a_late_ref, b_late_ref, factors_ref, out_ref):
    real, imag = rows_of(x_ref)
    pairs = ((1, 6), (2, 5), (3, 4))
    real, imag = exchanged(real, pairs), exchanged(imag, pairs)
    order = [((v << 1) & 15) | (v >> 3) for v in range(VREGS)]
    real, imag = [real[o] for o in order], [imag[o] for o in order]
    real, imag = cross(real, imag, factors_of(factors_ref, 0), 6, 6)
    real, imag = pair_op(times_on_lanes, (a_ref[0], a_ref[1]), real, imag)
    real, imag = pair_op(times_on_rows, (b_ref[0], b_ref[1]), real, imag)
    real, imag = cross(real, imag, factors_of(factors_ref, 1), 6, 6)
    real, imag = pair_op(times_on_rows, (b_late_ref[0], b_late_ref[1]), real, imag)
    real, imag = pair_op(times_on_lanes_transposed, (a_late_ref[0], a_late_ref[1]), real, imag)
    real, imag = cross(real, imag, factors_of(factors_ref, 2), 6, 6)
    for v in range(VREGS):
        three, q20, q19, q18 = v & 1, (v >> 1) & 1, (v >> 2) & 1, v >> 3
        at = 32 * (8 * three + 4 * q20 + 2 * q19 + q18) + 16
        out_ref[at : at + 8, :] = real[v]
        out_ref[at + 8 : at + 16, :] = imag[v]
    for three in range(2):
        for part in range(2):
            for low in range(SUBLANES):
                to = 32 * (8 * three + low) + 8 * part
                rows = out_ref[pl.ds(256 * three + 16 + 8 * part + low, SUBLANES, stride=32), :]
                out_ref[to : to + 8, :] = rows


def stage_three(x_ref, d_ref, state_hbm, marginal_hbm, state_ref, marginal_ref, semaphores):
    copies = (
        pltpu.make_async_copy(state_ref, state_hbm, semaphores.at[0]),
        pltpu.make_async_copy(marginal_ref, marginal_hbm, semaphores.at[1]),
    )
    for layout in range(2):
        at = [32 * v + 16 * layout for v in range(VREGS)]
        real = [x_ref[a : a + 8, :] for a in at]
        imag = [x_ref[a + 8 : a + 16, :] for a in at]
        for pairs in (((3, 6), (2, 2)), ((1, 1), (0, 0))):
            real, imag = exchanged(real, pairs), exchanged(imag, pairs)
        real, imag = pair_op(times_on_lanes, (d_ref[0], d_ref[1]), real, imag)
        for v in range(VREGS):
            if layout == 0:
                state_ref[pl.ds(2 * v, SUBLANES, stride=32), :] = real[v]
                state_ref[pl.ds(2 * v + 1, SUBLANES, stride=32), :] = imag[v]
            else:
                prob = real[v] * real[v] + imag[v] * imag[v]
                marginal_ref[v : v + 1, :] = jnp.sum(prob, axis=0, keepdims=True)
        copies[layout].start()
    for copy in copies:
        copy.wait()


INTERPRET = False
VMEM_LIMIT = 8 << 20
HBM = pl.BlockSpec(memory_space=pltpu.HBM)
VMEM = pl.BlockSpec(memory_space=pltpu.VMEM)


def run(kernel, outs, args, ins, out_specs, scratch=(), flops=1000000):
    return pl.pallas_call(
        kernel,
        out_shape=outs,
        in_specs=ins,
        out_specs=out_specs,
        scratch_shapes=scratch,
        compiler_params=pltpu.CompilerParams(vmem_limit_bytes=VMEM_LIMIT),
        cost_estimate=pl.CostEstimate(flops=flops, bytes_accessed=262144, transcendentals=0),
        name=kernel.__name__,
        interpret=INTERPRET,
    )(*args)


def array(*shape, dtype=jnp.float32):
    return jax.ShapeDtypeStruct(shape, dtype)


def first(x, gates):
    scratch = [pltpu.VMEM(x.shape, jnp.float32), pltpu.VMEM(gates.shape, jnp.float32), pltpu.SemaphoreType.DMA((2,))]
    args = (x, gates) if INTERPRET else tuple(pltpu.with_memory_space_constraint(a, pltpu.HBM) for a in (x, gates))
    return run(stage_one, array(2 * LANES, LANES), args, [HBM, HBM], VMEM, scratch)


def prepare(gates, after):
    lane = array(2, 2 * LANES, 2 * LANES, dtype=jnp.bfloat16)
    row = array(2, LANES, 2 * LANES, dtype=jnp.bfloat16)
    outs = [lane, row, lane, row, lane, array(3 * LANES, LANES)]
    ins = [VMEM, VMEM]
    return run(operators, outs, (gates, after), ins, [VMEM] * 6, flops=100000000)


def second(x, a, b, a_late, b_late, factors):
    return run(stage_two, array(4 * LANES, LANES), (x, a, b, a_late, b_late, factors), [VMEM] * 6, VMEM)


def third(x, d):
    outs = [array(2 * LANES, LANES), array(VREGS, LANES)]
    scratch = [pltpu.VMEM(out.shape, jnp.float32) for out in outs] + [pltpu.SemaphoreType.DMA((2,))]
    return run(stage_three, outs, (x, d), [VMEM, VMEM], [HBM, HBM], scratch)


def local(state, gates):
    amplitudes = state.shape[-1]
    rows = amplitudes // LANES
    matrices = gates.transpose(1, 2, 3, 4, 0).reshape(-1, gates.shape[0])
    x = state.reshape(2, rows, LANES).transpose(1, 0, 2).reshape(2 * rows, LANES)
    x = first(x, matrices)
    *two, d, factors = prepare(matrices, x)
    x = lax.all_to_all(x, ("high", "core", "narrow"), 0, 0, tiled=True)
    x = second(x, *two, factors)
    x = lax.all_to_all(x, ("core", "narrow"), 0, 0, tiled=True)
    final, marginal = third(x, d)
    final = final.reshape(rows, 2, LANES).transpose(1, 0, 2)
    return final.reshape(1, 1, 2, amplitudes), marginal.reshape(1, -1)


def solution(mesh):
    slices, wide, narrow = mesh.devices.shape
    devices = mesh.devices.reshape(slices, wide // 2, 2, narrow)
    split = Mesh(devices, ("slices", "high", "core", "narrow"))
    over_wide = ("slices", "high", "core")
    spec = P(over_wide, "narrow", None, None)
    return jax.shard_map(
        local, mesh=split, in_specs=(spec, P()), out_specs=(spec, P(over_wide, "narrow")), check_vma=False
    )
```

time: 61.3 us -> 60.9 us (level)
  blocking collectives: 52 us -> 12.4 us
  starting transfers between devices: 0 us -> 27.7 us
  waiting for transfers between devices: 0 us -> 10.4 us
  Pallas kernels: 6.45 us -> 8.94 us
  local copies, waits for them, and re-layouts: 1.8 us -> 0.01 us
    all_to_all x1 -> x0, blocking collectives: 39.2 us -> none  [local(): x = lax.all_to_all(x, ('high', 'core', 'narrow'), 0, 0, tiled=True)]
    all_to_all x0 -> x1, starting transfers between devices: none -> 27.7 us  [local(): x = lax.all_to_all(x, ('high', 'core', 'narrow'), 0, 0, tiled=True)]
    all_to_all x0 -> x1, waiting for transfers between devices: none -> 10.4 us  [local(): x = lax.all_to_all(x, ('high', 'core', 'narrow'), 0, 0, tiled=True)]
    pallas_call x3 -> x4, Pallas kernels: 6.45 us -> 8.94 us  [run(): pl.pallas_call(kernel, out_shape=outs, in_specs=ins, out_specs=out_specs,...]
    unnamed x6 -> x2, local copies, waits for them, and re-layouts: 1.8 us -> 0.01 us
  transfers between devices with their start and end apart: 0 -> 1, of which waited for: 0 -> 1; matrix products, arithmetic and copies ran while one was open for 0% -> 0% of each run, Pallas kernels for 0% -> 3%
where the time goes in v2:
time: 60.9 us; the launch traced here: 60.1 us
  starting transfers between devices  27.7 us (45%)
  blocking collectives  12.4 us (20%)
  waiting for transfers between devices  10.4 us (17%)
  Pallas kernels  8.94 us (15%)
  between operations  0.67 us (1%)
    all_to_all x1, starting transfers between devices, local(): x = lax.all_to_all(x, ('high', 'core', 'narrow'), 0, 0, tiled=True)  27.7 us
    all_to_all x1, blocking collectives, local(): x = lax.all_to_all(x, ('core', 'narrow'), 0, 0, tiled=True)  12.4 us
    all_to_all x1, waiting for transfers between devices, local(): x = lax.all_to_all(x, ('high', 'core', 'narrow'), 0, 0, tiled=True)  10.4 us
    pallas_call x4, Pallas kernels, run(): pl.pallas_call(kernel, out_shape=outs, in_specs=ins, out_specs=out_specs,...  8.94 us
  transfers between devices with their start and end apart: 1, of which 1 were waited for; matrix products, arithmetic and copies ran while one was open for 0% of the time, Pallas kernels for 3%

profile of v2, /device:TPU:513, one launch (start us, length us, event | category | flops | bytes accessed | tf_op | source)
XLA Modules:
  0.0 60.1 jit_solution(18387521139156167461)
XLA Ops:
  0.6 4.1 %stage_one.1.after_ref = f32[256,128]{1,0:T(8,128)} custom-call(f32[256,128]{1,0:T(8,128)} %bitcast.23, f32[224,8]{1,0:T(8,128)} %bitcast.21), custom_call_target="tpu_custom_call" | custom-call | flops 1000000 | bytes 262144 | tf_op jit(solution)/shard_map/stage_one/pallas_call | solution.py:421
  4.7 0.0 copy-start
  4.7 27.7 %all-to-all-start = ((f32[128,2,128]{2,1,0:T(2,128)}), f32[128,2,128]{2,1,0:T(2,128)S(1)}, u32[]{:S(2)}, u32[]{:S(2)}) async-start(f32[128,2,128]{2,1,0:T(2,128)} %bitcast.5), calls=%async_computation | async-start | bytes 262144 | tf_op jit(solution)/shard_map/all_to_all | solution.py:469
  32.5 0.0 copy-done
  32.5 1.8 %operators.1 = (bf16[2,256,256]{2,1,0:T(8,128)(2,1)S(1)}, bf16[2,128,256]{2,1,0:T(8,128)(2,1)S(1)}, bf16[2,256,256]{2,1,0:T(8,128)(2,1)S(1)}, bf16[2,128,256]{2,...) custom-call(f32[224,8]{1,0:T(8,128)S(1)} %bitcast.22, f32[256,128]{1,0:T(8,128)} %stage_one.1.after_ref), custom_call_target="tpu_custom_call" | custom-call | flops 100000000 | bytes 262144 | tf_op jit(solution)/shard_map/operators/pallas_call | solution.py:421
  34.2 10.4 %all-to-all-done = f32[128,2,128]{2,1,0:T(2,128)S(1)} async-done(((f32[128,2,128]{2,1,0:T(2,128)}), f32[128,2,128]{2,1,0:T(2,128)S(1)}, u32[]{:S(2)}, u32[]{:S(2)}) %all-to-all-start) | async-done | bytes 131104 | tf_op jit(solution)/shard_map/all_to_all | solution.py:469
  44.6 1.6 %stage_two.1 = f32[512,128]{1,0:T(8,128)S(1)} custom-call(f32[256,128]{1,0:T(8,128)S(1)} %bitcast.20, bf16[2,256,256]{2,1,0:T(8,128)(2,1)S(1)} %get-tuple-element.10.a_ref, bf16[2,128,256]{2,1,0:T(8,128)(2,1)S(1)} %get-tuple-element.11.b_ref, bf16[2,256,256]{2,1,0:T(8,128)(2,1)S(1)} %get-tuple-element.12.a_late_ref, ...), custom_call_target="tpu_custom_call" | custom-call | flops 1000000 | bytes 262144 | tf_op jit(solution)/shard_map/stage_two/pallas_call | solution.py:421
  46.2 12.4 %all_to_all.22 = f32[16,32,128]{2,1,0:T(8,128)S(1)} all-to-all(f32[16,32,128]{2,1,0:T(8,128)S(1)} %bitcast.19), channel_id=1, replica_groups=mesh['slices'=2,'high'=8,'core'=2,'narrow'=8] {'core','narrow'}, dimensions={0} | all-to-all | bytes 524288 | tf_op jit(solution)/shard_map/all_to_all | solution.py:471
  58.7 1.5 %stage_three.1 = (f32[256,128]{1,0:T(8,128)}, f32[16,128]{1,0:T(8,128)}) custom-call(f32[512,128]{1,0:T(8,128)S(1)} %bitcast.18, bf16[2,256,256]{2,1,0:T(8,128)(2,1)S(1)} %get-tuple-element.15.d_ref), custom_call_target="tpu_custom_call" | custom-call | flops 1000000 | bytes 262144 | tf_op jit(solution)/shard_map/stage_three/pallas_call | solution.py:421
Async XLA Ops:
  4.7 27.7 %copy-start = (f32[8,7,2,4,4]{0,4,3,2,1:T(4,128)S(1)}, f32[8,7,2,4,4]{0,4,3,2,1:T(4,128)}, u32[]{:S(2)}) copy-start(f32[8,7,2,4,4]{0,4,3,2,1:T(4,128)} %param.3) | copy-start | bytes 21508
  4.7 39.9 %all-to-all-start = ((f32[128,2,128]{2,1,0:T(2,128)}), f32[128,2,128]{2,1,0:T(2,128)S(1)}, u32[]{:S(2)}, u32[]{:S(2)}) async-start(f32[128,2,128]{2,1,0:T(2,128)} %bitcast.5), calls=%async_computation | async-start | bytes 262144 | tf_op jit(solution)/shard_map/all_to_all | solution.py:469
